TPU v7x, 256 devices: a whole 4x4x8 slice. The times are simulated.
256 devices in a mesh: ens: 8 (over z_hi, y), gy: 4 (over z_lo), gx: 8 (over x, core).
Axes of the slice: x: 4, y: 4, z: 8 (z_hi: 2, z_lo: 4; z = z_hi * 4 + z_lo), core: 2. Of those that a mesh axis runs over, the one named last changes fastest.
Arguments:
- velocity: float32 [8, 2, 1024, 2048], P('ens', None, 'gy', 'gx'), may hold values from -3 to 3
- stress: float32 [8, 3, 1024, 2048], P('ens', None, 'gy', 'gx'), may hold values from -3 to 3
- thickness: float32 [8, 1024, 2048], P('ens', 'gy', 'gx'), may hold values from 2 to 3
- concentration: float32 [8, 1024, 2048], P('ens', 'gy', 'gx'), may hold values from 0.97 to 1
- node_mass: float32 [8, 1024, 2048], P('ens', 'gy', 'gx'), may hold values from 1 to 1.5
- wind_stress: float32 [8, 2, 1024, 2048], P('ens', None, 'gy', 'gx'), may hold values from -3 to 3
- ocean_current: float32 [8, 2, 1024, 2048], P('ens', None, 'gy', 'gx'), may hold values from -2 to 2
- ocean_mask: int32 [1024, 2048], P('gy', 'gx'), may hold values 0 or 1
- ice_blocks: int32 [8, 32, 64], P('ens', 'gy', 'gx'), may hold values 0 or 1
Outputs:
- velocity_out: float32 [8, 2, 1024, 2048], P('ens', None, 'gy', 'gx')
- stress_out: float32 [8, 3, 1024, 2048], P('ens', None, 'gy', 'gx')
- ensemble_mean: float32 [3, 1024, 2048], P(None, ('gy', 'ens'), 'gx')
- ensemble_variance: float32 [3, 1024, 2048], P(None, ('gy', 'ens'), 'gx')
All inputs are finite; a program needn't handle non-finite values. No bound on the sum of `ocean_mask` or of `ice_blocks` on one device may be relied on, other than what follows from the above.
Results may differ from a plain program's by a relative error of at most 0.00002.
Values sent between devices are 32-bit elements; how exact they have to be, the bound alone decides.
A program may use at most 64 MiB of HBM per device.

v0:
```python
import functools
import math

import jax
import jax.numpy as jnp
from jax import lax
from jax.experimental import pallas as pl
from jax.experimental.pallas import tpu as pltpu
from jax.sharding import PartitionSpec as P

SUBCYCLES = 16
RELAX = 0.25
DECAY = 20.0
FLOOR = 0.5
ROOT2 = math.sqrt(2.0)
BETA = 1.0 / (4.0 * ROOT2)
KEEP = 1.0 / (1.0 + RELAX)
GAIN = BETA * 0.5 * RELAX * KEEP
TINY = 1.1754944e-38

LANES = 128
ROWS = 256
BASE = 24
HALO = 16
ALLOC = 312
FIRST, LAST = 1, 37
W, Z, PP, MM, TT, SM, MA, WW, WZ, CW, CZ, B2, BB = range(13)
SENT = 12
PITCH = 20
LAG = 8
MESH_IDS = pl.DeviceIdType.MESH


def lane_ids():
    return lax.broadcasted_iota(jnp.int32, (8, LANES), 1)


def tile(r):
    return pl.ds(r, 8)


def sweep(F, RL, tiles, first, last, lag):
    lane = lane_ids()
    low, high = lane == 0, lane == LANES - 1

    def ld(f, q, r):
        return F[f, q, tile(r), :]

    def rl(f, q, r):
        return RL[f, q, tile(r), :]

    def turn(dst, src, t, shift, edge):
        values = [pltpu.roll(ld(src, q, 8 * t), shift, 1) for q in tiles]
        if len(tiles) == 2:
            values = [jnp.where(edge, values[1 - n], values[n]) for n in range(2)]
        for q, value in zip(tiles, values):
            RL[dst, q, tile(8 * t), :] = value

    def stress(t):
        r = 8 * t
        for q in tiles:
            w, wd = ld(W, q, r), ld(W, q, r + 1)
            z, zd = ld(Z, q, r), ld(Z, q, r + 1)
            w1, w1d = rl(0, q, r), rl(0, q, r + 1)
            z1, z1d = rl(1, q, r), rl(1, q, r + 1)
            a, b, c, d = w1d - w, z1 - zd, z1d - z, w1 - wd
            div, shear, tension = a + b, a - b, c + d
            s4, t4 = shear * 0.25, tension * 0.25
            square = div * div + (shear * s4 + tension * t4)
            inverse = lax.rsqrt(jnp.maximum(square, TINY))
            e = div - square * inverse
            g = ld(SM, q, r) * jnp.minimum(inverse, 1.0 / FLOOR)
            F[PP, q, tile(r), :] = ld(PP, q, r) * KEEP + g * (e + s4)
            F[MM, q, tile(r), :] = ld(MM, q, r) * KEEP + g * (e - s4)
            F[TT, q, tile(r), :] = ld(TT, q, r) * KEEP + g * t4
        for dst, src in ((2, PP), (3, MM), (4, TT)):
            turn(dst, src, t, 1, low)

    def momentum(t):
        r = 8 * t
        for q in tiles:
            fw = (ld(PP, q, r) - rl(2, q, r - 1)) + (ld(TT, q, r - 1) - rl(4, q, r))
            fz = (ld(TT, q, r) - rl(4, q, r - 1)) + (ld(MM, q, r - 1) - rl(3, q, r))
            w, z = ld(W, q, r), ld(Z, q, r)
            cw, cz = ld(CW, q, r), ld(CZ, q, r)
            dw, dz = cw - w, cz - z
            dq = dw * dw + dz * dz
            drag = dq * lax.rsqrt(jnp.maximum(dq, TINY))
            mass, b = ld(MA, q, r), ld(BB, q, r)
            a = mass + drag
            rw = (mass * w + drag * cw) + (fw + ld(WW, q, r))
            rz = (mass * z + drag * cz) + (fz + ld(WZ, q, r))
            root = lax.rsqrt(a * a + ld(B2, q, r))
            quotient = root * root
            a, b = a * quotient, b * quotient
            F[W, q, tile(r), :] = a * rw - b * rz
            F[Z, q, tile(r), :] = a * rz + b * rw
        for dst, src in ((0, W), (1, Z)):
            turn(dst, src, t, LANES - 1, high)

    for k in range(last - first + lag):
        if first + k < last:
            stress(first + k)
        if k >= lag:
            momentum(first + k - lag)


def kernel(
    vel_h, st_h, thick_h, conc_h, mass_h, wind_h, cur_h, mask_h, ice_s,
    vel_o, st_o, conc_o,
    F, RL, IN, MK, SP, RP, OUT,
    load_sem, send_sem, recv_sem, out_sem,
):
    gx, gy = lax.axis_index("gx"), lax.axis_index("gy")
    nx, ny = lax.axis_size("gx"), lax.axis_size("gy")
    left, right = lax.rem(gx + nx - 1, nx), lax.rem(gx + 1, nx)
    has_down, has_up = gy > 0, gy < ny - 1
    lane = lane_ids()
    halves = (pl.ds(0, LANES), pl.ds(LANES, LANES))
    whole = pl.ds(0, ROWS)

    sources = [vel_h.at[0, 0], vel_h.at[0, 1], st_h.at[0, 0], st_h.at[0, 1], st_h.at[0, 2],
               thick_h.at[0], conc_h.at[0], mass_h.at[0], wind_h.at[0, 0], wind_h.at[0, 1],
               cur_h.at[0, 0], cur_h.at[0, 1]]
    loads = []
    for n, source in enumerate(sources):
        for q in range(2):
            loads.append(pltpu.make_async_copy(
                source.at[whole, halves[q]], IN.at[n, q], load_sem.at[2 * n + q]))
    for q in range(2):
        loads.append(pltpu.make_async_copy(
            mask_h.at[whole, halves[q]], MK.at[q], load_sem.at[24 + q]))
    for copy in loads:
        copy.start()

    barrier = pltpu.get_barrier_semaphore()
    for neighbour in (left, right):
        pl.semaphore_signal(barrier, inc=1, device_id={"gx": neighbour}, device_id_type=MESH_IDS)

    @pl.when(has_down)
    def _():
        pl.semaphore_signal(barrier, inc=1, device_id={"gy": gy - 1}, device_id_type=MESH_IDS)

    @pl.when(has_up)
    def _():
        pl.semaphore_signal(barrier, inc=1, device_id={"gy": gy + 1}, device_id_type=MESH_IDS)

    zero = jnp.zeros((8, LANES), jnp.float32)
    for f in (PP, MM, TT):
        for q in range(3):
            F[f, q, tile(0), :] = zero
    for f in (2, 3, 4):
        for q in range(3):
            RL[f, q, tile(0), :] = zero

    for copy in loads:
        copy.wait()

    def slot_mask(start, width):
        return lax.rem(lane - start + 2 * LANES, LANES) < width

    def derive(block, carry):
        present = []
        for q in range(2):
            c = [ice_s[0, block, 4 * q + n] for n in range(4)]
            present.append(jnp.where(
                lane < 64, jnp.where(lane < 32, c[0], c[1]), jnp.where(lane < 96, c[2], c[3])))
        for n in range(4):
            r = pl.multiple_of(block * 32 + 8 * n, 8)
            fields = []
            for q in range(2):
                u, v, s0, s1, s2, thick, conc, mass, we, wn, ce, cn = (
                    IN[f, q, tile(r), :] for f in range(12))
                active = (MK[q, tile(r), :] * present[q]).astype(jnp.float32)
                u, v = u * active, v * active
                strength = thick * jnp.exp(-DECAY * (1.0 - conc))
                s0, s2 = s0 * BETA, s2 * (2.0 * BETA)
                scale = 0.5 / ROOT2
                fields.append((
                    0.5 * (u + v), 0.5 * (u - v), s0 + s2, s0 - s2, s1 * BETA, strength * GAIN,
                    mass * ROOT2, scale * (we + wn), scale * (we - wn),
                    0.5 * (ce + cn), 0.5 * (ce - cn), active))
                for f in range(SENT):
                    F[f, q, tile(r + BASE), :] = fields[q][f]
            for part in range(2):
                to_left = to_right = None
                for s in range(6):
                    f = 6 * part + s
                    low = pltpu.roll(fields[0][f], PITCH * s, 1) if s else fields[0][f]
                    high = pltpu.roll(fields[1][f], (PITCH * s + 33) % LANES, 1)
                    if s == 0:
                        to_left, to_right = low, high
                    else:
                        to_left = jnp.where(slot_mask(PITCH * s, 17), low, to_left)
                        to_right = jnp.where(slot_mask(PITCH * s + 17, 16), high, to_right)
                SP[0, part, tile(r), :] = to_left
                SP[1, part, tile(r), :] = to_right
        return carry

    lax.fori_loop(0, ROWS // 32, derive, 0)

    pl.semaphore_wait(barrier, 2 + has_down.astype(jnp.int32) + has_up.astype(jnp.int32))

    to_left = pltpu.make_async_remote_copy(
        SP.at[0], RP.at[0], send_sem.at[0], recv_sem.at[0],
        device_id={"gx": left}, device_id_type=MESH_IDS)
    to_right = pltpu.make_async_remote_copy(
        SP.at[1], RP.at[1], send_sem.at[1], recv_sem.at[1],
        device_id={"gx": right}, device_id_type=MESH_IDS)
    to_left.start()
    to_right.start()

    def row_copies(q, count, n):
        planes = pl.ds(q, count)

        def part(f0, nf, src, dst, rows, slot, row):
            return pltpu.make_async_remote_copy(
                F.at[pl.ds(f0, nf), planes, pl.ds(src, rows)],
                F.at[pl.ds(f0, nf), planes, pl.ds(dst, rows)],
                send_sem.at[slot], recv_sem.at[slot],
                device_id={"gy": row}, device_id_type=MESH_IDS)

        down = [part(0, SENT, BASE, BASE + ROWS, HALO, n, gy - 1),
                part(0, 2, BASE + HALO, BASE + ROWS + HALO, 8, n + 1, gy - 1)]
        up = [part(0, SENT, BASE + ROWS - HALO, BASE - HALO, HALO, n + 2, gy + 1)]
        return down, up

    main_down, main_up = row_copies(0, 2, 2)
    strip_down, strip_up = row_copies(2, 1, 5)

    def start_rows(down, up):
        @pl.when(has_down)
        def _():
            for copy in down:
                copy.start()

        @pl.when(has_up)
        def _():
            for copy in up:
                copy.start()

    def wait_rows(down, up):
        @pl.when(has_down)
        def _():
            for copy in down:
                copy.wait_send()
            for copy in up:
                copy.wait_recv()

        @pl.when(has_up)
        def _():
            for copy in up:
                copy.wait_send()
            for copy in down:
                copy.wait_recv()

    start_rows(main_down, main_up)
    to_left.wait_recv()
    to_right.wait_recv()

    def build(block, carry):
        for n in range(2):
            r = pl.multiple_of(block * 16 + 8 * n, 8)
            for part in range(2):
                from_right, from_left = RP[0, part, tile(r), :], RP[1, part, tile(r), :]
                for s in range(6):
                    f = 6 * part + s
                    both = jnp.where(slot_mask(PITCH * s + 17, 16), from_left, from_right)
                    both = pltpu.roll(both, (95 - PITCH * s) % LANES, 1)
                    high = pltpu.roll(F[f, 1, tile(r + BASE), :], 95, 1)
                    F[f, 2, tile(r + BASE), :] = jnp.where(
                        lane < 48, F[f, 0, tile(r + BASE), :], jnp.where(lane < 95, high, both))
        return carry

    lax.fori_loop(0, ROWS // 16, build, 0)
    start_rows(strip_down, strip_up)

    def outside(start, count):
        for f in range(SENT):
            value = jnp.ones((8, LANES), jnp.float32) if f == MA else zero
            for q in range(3):
                for n in range(count):
                    F[f, q, tile(start + 8 * n), :] = value

    @pl.when(jnp.logical_not(has_down))
    def _():
        outside(BASE - HALO, 2)

    @pl.when(jnp.logical_not(has_up))
    def _():
        outside(BASE + ROWS, 3)

    to_left.wait_send()
    to_right.wait_send()
    wait_rows(main_down, main_up)
    wait_rows(strip_down, strip_up)

    sub = lax.broadcasted_iota(jnp.int32, (8, LANES), 0)
    grid_rows = ny * ROWS

    def prepare(t, carry):
        r = pl.multiple_of(8 * t, 8)
        row = (sub + (gy * ROWS - BASE + r)).astype(jnp.float32) + 0.5
        half = row * (0.5 / grid_rows)
        for q in range(3):
            b = half * F[MA, q, tile(r), :]
            F[BB, q, tile(r), :] = b
            F[B2, q, tile(r), :] = jnp.where(F[B2, q, tile(r), :] > 0.5, b * b, jnp.inf)
        return carry

    lax.fori_loop(FIRST, LAST, prepare, 0)

    def turn_first(t, carry):
        r = pl.multiple_of(8 * t, 8)
        for dst, f in ((0, W), (1, Z)):
            v = [pltpu.roll(F[f, q, tile(r), :], LANES - 1, 1) for q in range(3)]
            RL[dst, 0, tile(r), :] = jnp.where(lane == LANES - 1, v[1], v[0])
            RL[dst, 1, tile(r), :] = jnp.where(lane == LANES - 1, v[0], v[1])
            RL[dst, 2, tile(r), :] = v[2]
        return carry

    lax.fori_loop(FIRST, LAST + 1, turn_first, 0)

    def main_cycle(n, carry):
        sweep(F, RL, (0, 1), FIRST, LAST, LAG)
        return carry

    def strip_cycle(n, carry):
        sweep(F, RL, (2,), FIRST, LAST, LAG)
        return carry

    lax.fori_loop(0, SUBCYCLES, main_cycle, 0)
    lax.fori_loop(0, SUBCYCLES, strip_cycle, 0)

    def finish(block, carry):
        for n in range(2):
            o = pl.multiple_of(block * 16 + 8 * n, 8)
            r = o + BASE

            def merged(values):
                low = jnp.where(lane < 16, values[2], values[0])
                high = jnp.where(lane >= 108, pltpu.roll(values[2], 33, 1), values[1])
                return low, high

            div = []
            for q in range(3):
                a = RL[0, q, tile(r + 1), :] - F[W, q, tile(r), :]
                b = RL[1, q, tile(r), :] - F[Z, q, tile(r + 1), :]
                div.append(a + b)
            div = merged(div)
            w, z, p, m, t = (
                merged([F[f, q, tile(r), :] for q in range(3)]) for f in (W, Z, PP, MM, TT))
            for q in range(2):
                conc = IN[6, q, tile(o), :]
                OUT[0, q, tile(o), :] = w[q] + z[q]
                OUT[1, q, tile(o), :] = w[q] - z[q]
                OUT[2, q, tile(o), :] = (p[q] + m[q]) * (0.5 / BETA)
                OUT[3, q, tile(o), :] = t[q] * (1.0 / BETA)
                OUT[4, q, tile(o), :] = (p[q] - m[q]) * (0.25 / BETA)
                OUT[5, q, tile(o), :] = jnp.clip(conc - conc * div[q], 0.0, 1.0)
        return carry

    lax.fori_loop(0, ROWS // 16, finish, 0)
    targets = [vel_o.at[0, 0], vel_o.at[0, 1], st_o.at[0, 0], st_o.at[0, 1], st_o.at[0, 2],
               conc_o.at[0]]
    stores = []
    for n, target in enumerate(targets):
        for q in range(2):
            stores.append(pltpu.make_async_copy(
                OUT.at[n, q], target.at[whole, halves[q]], out_sem.at[2 * n + q]))
    for copy in stores:
        copy.start()
    for copy in stores:
        copy.wait()


def body(velocity, stress, thickness, concentration, node_mass, wind_stress, ocean_current,
         ocean_mask, ice_blocks):
    f32 = jnp.float32
    anywhere = pl.BlockSpec(memory_space=pl.ANY)
    final_vel, final_stress, drifted = pl.pallas_call(
        kernel,
        out_shape=(
            jax.ShapeDtypeStruct(velocity.shape, f32),
            jax.ShapeDtypeStruct(stress.shape, f32),
            jax.ShapeDtypeStruct(concentration.shape, f32),
        ),
        in_specs=[anywhere] * 8 + [pl.BlockSpec(memory_space=pltpu.SMEM)],
        out_specs=(anywhere,) * 3,
        scratch_shapes=[
            pltpu.VMEM((13, 3, ALLOC, LANES), f32),
            pltpu.VMEM((5, 3, ALLOC, LANES), f32),
            pltpu.VMEM((12, 2, ROWS, LANES), f32),
            pltpu.VMEM((2, ROWS, LANES), jnp.int32),
            pltpu.VMEM((2, 2, ROWS, LANES), f32),
            pltpu.VMEM((2, 2, ROWS, LANES), f32),
            pltpu.VMEM((6, 2, ROWS, LANES), f32),
            pltpu.SemaphoreType.DMA((26,)),
            pltpu.SemaphoreType.DMA((8,)),
            pltpu.SemaphoreType.DMA((8,)),
            pltpu.SemaphoreType.DMA((12,)),
        ],
        compiler_params=pltpu.CompilerParams(
            collective_id=0, has_side_effects=True, vmem_limit_bytes=67043328),
        name="ice",
    )(velocity, stress, thickness, concentration, node_mass, wind_stress, ocean_current,
      ocean_mask, ice_blocks)
    fields = jnp.stack([drifted, final_vel[:, 0], final_vel[:, 1]], axis=1)
    members = lax.axis_size("ens")
    gathered = lax.all_to_all(fields, "ens", split_axis=2, concat_axis=0, tiled=True)
    mean = jnp.sum(gathered, axis=0) / members
    deviation = gathered - mean[None]
    spread = jnp.sum(deviation * deviation, axis=0) / members
    return final_vel, final_stress, mean, spread


def solution(mesh):
    member, field = P("ens", None, "gy", "gx"), P("ens", "gy", "gx")
    placed = (member, member, field, field, field, member, member, P("gy", "gx"), field)
    block = P(None, ("gy", "ens"), "gx")
    return jax.shard_map(
        body, mesh=mesh, in_specs=placed, out_specs=(member, member, block, block),
        check_vma=False)
```

profile of v0, /device:TPU:32, one launch (start us, length us, event | category | flops | bytes accessed | tf_op | source)
XLA Modules:
  0.0 83.1 jit_solution(3820244084126098178)
XLA Ops:
  0.6 44.0 %ice.1 = (f32[1,2,256,256]{3,2,1,0:T(8,128)}, f32[1,3,256,256]{3,2,1,0:T(8,128)}, f32[1,256,256]{2,1,0:T(8,128)}) custom-call(f32[1,2,256,256]{3,2,1,0:T(8,128)} %vel_h.1, f32[1,3,256,256]{3,2,1,0:T(8,128)} %st_h.1, f32[1,256,256]{2,1,0:T(8,128)} %thick_h.1, f32[1,256,256]{2,1,0:T(8,128)} %conc_h.1, f32[1,256,256]{2,1,0:T(8,128)} %mass_h.1, ...), custom_call_target="tpu_custom_call" | custom-call | tf_op jit(solution)/shard_map/ice/pallas_call | solution.py:381
  44.6 1.2 %pad_maximum_fusion = f32[1,3,256,256]{3,2,1,0:T(8,128)S(1)} fusion(f32[1,2,256,256]{3,2,1,0:T(8,128)} %get-tuple-element.22, f32[1,1,256,256]{3,2,1,0:T(8,128)} %bitcast.8), kind=kLoop, calls=%fused_computation | loop fusion | flops 196608 | bytes 1572864 | tf_op jit(solution)/shard_map/stack | solution.py:408
  45.8 1.7 %copy.18 = f32[1,3,256,256]{3,0,1,2:T(1,128)} copy(f32[1,3,256,256]{3,2,1,0:T(8,128)S(1)} %pad_maximum_fusion) | data formatting | bytes 1572864 | tf_op jit(solution)/shard_map/stack | solution.py:408
  47.5 9.3 %all-to-all-start = ((f32[1,3,256,256]{3,0,1,2:T(1,128)}), f32[1,3,256,256]{3,0,1,2:T(1,128)S(1)}, u32[]{:S(2)}, u32[]{:S(2)}) async-start(f32[1,3,256,256]{3,0,1,2:T(1,128)} %copy.18), calls=%async_computation | async-start | bytes 1572864 | tf_op jit(solution)/shard_map/all_to_all | solution.py:410
  56.8 23.2 %all-to-all-done = f32[1,3,256,256]{3,0,1,2:T(1,128)S(1)} async-done(((f32[1,3,256,256]{3,0,1,2:T(1,128)}), f32[1,3,256,256]{3,0,1,2:T(1,128)S(1)}, u32[]{:S(2)}, u32[]{:S(2)}) %all-to-all-start) | async-done | bytes 786464 | tf_op jit(solution)/shard_map/all_to_all | solution.py:410
  80.0 0.1 copy.19
  80.1 0.1 reduce_sum.18
  80.1 0.0 copy-start.2
  80.2 0.0 copy-start
  80.2 0.1 multiply_reduce_fusion
  80.3 0.5 copy-done.2
  80.8 0.0 copy-start.1
  80.8 0.6 broadcast_multiply_fusion
  81.4 0.0 copy-done
  81.4 0.8 copy.31
  82.2 0.0 copy-done.1
  82.2 0.9 %copy.32 = f32[1,3,256,256]{3,2,1,0:T(8,128)} copy(f32[1,3,256,256]{3,2,1,0:T(8,128)S(1)} %copy-done.1) | data formatting | bytes 1572864
  (1 shorter events, 0.0 us)
Async XLA Ops:
  47.5 32.5 %all-to-all-start = ((f32[1,3,256,256]{3,0,1,2:T(1,128)}), f32[1,3,256,256]{3,0,1,2:T(1,128)S(1)}, u32[]{:S(2)}, u32[]{:S(2)}) async-start(f32[1,3,256,256]{3,0,1,2:T(1,128)} %copy.18), calls=%async_computation | async-start | bytes 1572864 | tf_op jit(solution)/shard_map/all_to_all | solution.py:410
  80.1 0.6 copy-start.2
  80.2 1.3 %copy-start = (f32[1,2,256,256]{3,2,1,0:T(8,128)S(1)}, f32[1,2,256,256]{3,2,1,0:T(8,128)}, u32[]{:S(2)}) copy-start(f32[1,2,256,256]{3,2,1,0:T(8,128)} %get-tuple-element.22) | copy-start | bytes 1572868
  80.8 1.4 %copy-start.1 = (f32[1,3,256,256]{3,2,1,0:T(8,128)S(1)}, f32[1,3,256,256]{3,2,1,0:T(8,128)}, u32[]{:S(2)}) copy-start(f32[1,3,256,256]{3,2,1,0:T(8,128)} %get-tuple-element.23) | copy-start | bytes 2359300
where the time goes:
time: 83.3 us; the launch traced here: 83.1 us
  Pallas kernels  44 us (53%)
  waiting for transfers between devices  23.2 us (28%)
  starting transfers between devices  9.3 us (11%)
  local copies, waits for them, and re-layouts  3.96 us (5%)
  other arithmetic  1.96 us (2%)
    pallas_call x1, Pallas kernels, body(): pl.pallas_call(kernel, out_shape=(jax.ShapeDtypeStruct(velocity.shape, f3...  44 us
    all_to_all x1, waiting for transfers between devices, body(): lax.all_to_all(fields, 'ens', split_axis=2, concat_axis=0, tiled=True)  23.2 us
    all_to_all x1, starting transfers between devices, body(): lax.all_to_all(fields, 'ens', split_axis=2, concat_axis=0, tiled=True)  9.3 us
    unnamed x8, local copies, waits for them, and re-layouts  2.22 us
    another operation x1, local copies, waits for them, and re-layouts, body(): fields = jnp.stack([drifted, final_vel[:, 0], final_vel[:, 1]], axis=1)  1.69 us
  transfers between devices with their start and end apart: 1, of which 1 were waited for; matrix products, arithmetic and copies ran while one was open for 0% of the time, Pallas kernels for 0%

commit v1 on v0

--- a/solution.py
+++ b/solution.py
@@ -28,6 +28,11 @@
 SENT = 12
 PITCH = 20
 LAG = 8
+EARLY = 8
+CHUNK = 64
+CTILES = CHUNK // 8 + 2
+CLAG = 3
+OWN = 32
 MESH_IDS = pl.DeviceIdType.MESH
 
 
@@ -39,22 +44,26 @@
     return pl.ds(r, 8)
 
 
-def sweep(F, RL, tiles, first, last, lag):
+def sweep(state, rolled, const, tiles, first, last, lag):
     lane = lane_ids()
     low, high = lane == 0, lane == LANES - 1
+    (S, so), (RL, ro), (C, co) = state, rolled, const
 
     def ld(f, q, r):
-        return F[f, q, tile(r), :]
+        return S[f, q, tile(r + so), :]
 
     def rl(f, q, r):
-        return RL[f, q, tile(r), :]
+        return RL[f, q, tile(r + ro), :]
+
+    def const_of(f, q, r):
+        return C[f, q, tile(r + co), :]
 
     def turn(dst, src, t, shift, edge):
         values = [pltpu.roll(ld(src, q, 8 * t), shift, 1) for q in tiles]
-        if len(tiles) == 2:
-            values = [jnp.where(edge, values[1 - n], values[n]) for n in range(2)]
+        if len(tiles) > 1:
+            values[:2] = [jnp.where(edge, values[1 - n], values[n]) for n in range(2)]
         for q, value in zip(tiles, values):
-            RL[dst, q, tile(8 * t), :] = value
+            RL[dst, q, tile(8 * t + ro), :] = value
 
     def stress(t):
         r = 8 * t
@@ -69,10 +78,10 @@
             square = div * div + (shear * s4 + tension * t4)
             inverse = lax.rsqrt(jnp.maximum(square, TINY))
             e = div - square * inverse
-            g = ld(SM, q, r) * jnp.minimum(inverse, 1.0 / FLOOR)
-            F[PP, q, tile(r), :] = ld(PP, q, r) * KEEP + g * (e + s4)
-            F[MM, q, tile(r), :] = ld(MM, q, r) * KEEP + g * (e - s4)
-            F[TT, q, tile(r), :] = ld(TT, q, r) * KEEP + g * t4
+            g = const_of(SM, q, r) * jnp.minimum(inverse, 1.0 / FLOOR)
+            S[PP, q, tile(r + so), :] = ld(PP, q, r) * KEEP + g * (e + s4)
+            S[MM, q, tile(r + so), :] = ld(MM, q, r) * KEEP + g * (e - s4)
+            S[TT, q, tile(r + so), :] = ld(TT, q, r) * KEEP + g * t4
         for dst, src in ((2, PP), (3, MM), (4, TT)):
             turn(dst, src, t, 1, low)
 
@@ -82,19 +91,19 @@
             fw = (ld(PP, q, r) - rl(2, q, r - 1)) + (ld(TT, q, r - 1) - rl(4, q, r))
             fz = (ld(TT, q, r) - rl(4, q, r - 1)) + (ld(MM, q, r - 1) - rl(3, q, r))
             w, z = ld(W, q, r), ld(Z, q, r)
-            cw, cz = ld(CW, q, r), ld(CZ, q, r)
+            cw, cz = const_of(CW, q, r), const_of(CZ, q, r)
             dw, dz = cw - w, cz - z
             dq = dw * dw + dz * dz
             drag = dq * lax.rsqrt(jnp.maximum(dq, TINY))
-            mass, b = ld(MA, q, r), ld(BB, q, r)
+            mass, b = const_of(MA, q, r), const_of(BB, q, r)
             a = mass + drag
-            rw = (mass * w + drag * cw) + (fw + ld(WW, q, r))
-            rz = (mass * z + drag * cz) + (fz + ld(WZ, q, r))
-            root = lax.rsqrt(a * a + ld(B2, q, r))
+            rw = (mass * w + drag * cw) + (fw + const_of(WW, q, r))
+            rz = (mass * z + drag * cz) + (fz + const_of(WZ, q, r))
+            root = lax.rsqrt(a * a + const_of(B2, q, r))
             quotient = root * root
             a, b = a * quotient, b * quotient
-            F[W, q, tile(r), :] = a * rw - b * rz
-            F[Z, q, tile(r), :] = a * rz + b * rw
+            S[W, q, tile(r + so), :] = a * rw - b * rz
+            S[Z, q, tile(r + so), :] = a * rz + b * rw
         for dst, src in ((0, W), (1, Z)):
             turn(dst, src, t, LANES - 1, high)
 
@@ -107,9 +116,9 @@
 
 def kernel(
     vel_h, st_h, thick_h, conc_h, mass_h, wind_h, cur_h, mask_h, ice_s,
-    vel_o, st_o, conc_o,
-    F, RL, IN, MK, SP, RP, OUT,
-    load_sem, send_sem, recv_sem, out_sem,
+    vel_o, st_o, mean_o, var_o,
+    F, RL, IN, MK, SP, RP, OUT, G, FB, YR, PART, ZR, STAT,
+    load_sem, send_sem, recv_sem, out_sem, ysend_sem, yrecv_sem, zsend_sem, zrecv_sem,
 ):
     gx, gy = lax.axis_index("gx"), lax.axis_index("gy")
     nx, ny = lax.axis_size("gx"), lax.axis_size("gy")
@@ -144,6 +153,13 @@
     @pl.when(has_up)
     def _():
         pl.semaphore_signal(barrier, inc=1, device_id={"gy": gy + 1}, device_id_type=MESH_IDS)
+
+    ens = lax.axis_index("ens")
+    z_hi, y = ens // 4, lax.rem(ens, 4)
+    y_peers = [z_hi * 4 + lax.rem(y + d, 4) for d in (1, 2, 3)]
+    partner = (1 - z_hi) * 4 + y
+    for peer in y_peers + [partner]:
+        pl.semaphore_signal(barrier, inc=1, device_id={"ens": peer}, device_id_type=MESH_IDS)
 
     zero = jnp.zeros((8, LANES), jnp.float32)
     for f in (PP, MM, TT):
@@ -199,7 +215,7 @@
 
     lax.fori_loop(0, ROWS // 32, derive, 0)
 
-    pl.semaphore_wait(barrier, 2 + has_down.astype(jnp.int32) + has_up.astype(jnp.int32))
+    pl.semaphore_wait(barrier, 6 + has_down.astype(jnp.int32) + has_up.astype(jnp.int32))
 
     to_left = pltpu.make_async_remote_copy(
         SP.at[0], RP.at[0], send_sem.at[0], recv_sem.at[0],
@@ -321,56 +337,153 @@
 
     lax.fori_loop(FIRST, LAST + 1, turn_first, 0)
 
+    whole_state, whole_rolled, const = (F, 0), (RL, 0), (F, 0)
+
     def main_cycle(n, carry):
-        sweep(F, RL, (0, 1), FIRST, LAST, LAG)
+        sweep(whole_state, whole_rolled, const, (0, 1), FIRST, LAST, LAG)
         return carry
 
     def strip_cycle(n, carry):
-        sweep(F, RL, (2,), FIRST, LAST, LAG)
-        return carry
-
-    lax.fori_loop(0, SUBCYCLES, main_cycle, 0)
-    lax.fori_loop(0, SUBCYCLES, strip_cycle, 0)
-
-    def finish(block, carry):
-        for n in range(2):
-            o = pl.multiple_of(block * 16 + 8 * n, 8)
-            r = o + BASE
-
-            def merged(values):
-                low = jnp.where(lane < 16, values[2], values[0])
-                high = jnp.where(lane >= 108, pltpu.roll(values[2], 33, 1), values[1])
-                return low, high
-
+        sweep(whole_state, whole_rolled, const, (2,), FIRST, LAST, LAG)
+        return carry
+
+    lax.fori_loop(0, EARLY, main_cycle, 0)
+    lax.fori_loop(0, EARLY, strip_cycle, 0)
+
+    def merged(values):
+        low = jnp.where(lane < 16, values[2], values[0])
+        high = jnp.where(lane >= 108, pltpu.roll(values[2], 33, 1), values[1])
+        return low, high
+
+    def chunk_stores(i):
+        rows = pl.ds(CHUNK * i, CHUNK)
+        targets = [(FB.at[1], vel_o.at[0, 0]), (FB.at[2], vel_o.at[0, 1]), (OUT.at[0], st_o.at[0, 0]),
+                   (OUT.at[1], st_o.at[0, 1]), (OUT.at[2], st_o.at[0, 2])]
+        return [
+            pltpu.make_async_copy(
+                source.at[q, rows], target.at[rows, halves[q]], out_sem.at[10 * i + 2 * n + q])
+            for n, (source, target) in enumerate(targets) for q in range(2)]
+
+    def y_copy(i, d):
+        target = lax.rem(y + d, 4)
+        block = i // 2
+        rows = pl.ds(pl.multiple_of(CHUNK * i + OWN * lax.rem(target, 2), 8), OWN)
+        return target // 2 == i % 2, pltpu.make_async_remote_copy(
+            FB.at[:, :, rows], YR.at[block, 3 - d],
+            ysend_sem.at[3 * block + d - 1], yrecv_sem.at[3 * block + 3 - d],
+            device_id={"ens": y_peers[d - 1]}, device_id_type=MESH_IDS)
+
+    z_copy = pltpu.make_async_remote_copy(
+        PART.at[1 - z_hi], ZR, zsend_sem, zrecv_sem,
+        device_id={"ens": partner}, device_id_type=MESH_IDS)
+
+    def partial(i):
+        block = i // 2
+
+        @pl.when(y // 2 == i % 2)
+        def _():
+            for d in (1, 2, 3):
+                y_copy(i, d)[1].wait_recv()
+            own = CHUNK * i + OWN * lax.rem(y, 2)
+
+            def reduce(n, carry):
+                r = pl.multiple_of(8 * n, 8)
+                for f in range(3):
+                    for q in range(2):
+                        v = [YR[block, d, f, q, tile(r), :] for d in range(3)]
+                        v.append(FB[f, q, tile(pl.multiple_of(own + r, 8)), :])
+                        total = (v[0] + v[1]) + (v[2] + v[3])
+                        mean = total * 0.25
+                        e = [x - mean for x in v]
+                        PART[block, 0, f, q, tile(r), :] = total
+                        PART[block, 1, f, q, tile(r), :] = (
+                            (e[0] * e[0] + e[1] * e[1]) + (e[2] * e[2] + e[3] * e[3]))
+                return carry
+
+            lax.fori_loop(0, OWN // 8, reduce, 0)
+
+            @pl.when(z_hi != block)
+            def _():
+                z_copy.start()
+
+    order = (0, 2, 1, 3)
+    for place, i in enumerate(order):
+        base = BASE - 16 + CHUNK * i
+
+        def fetch(t, carry):
+            r = pl.multiple_of(8 * t, 8)
+            for q in range(3):
+                for f in range(5):
+                    G[f, q, tile(r), :] = F[f, q, tile(r + base), :]
+                    G[5 + f, q, tile(r), :] = RL[f, q, tile(r + base), :]
+            return carry
+
+        lax.fori_loop(0, CTILES + 2, fetch, 0)
+
+        def chunk_cycle(n, carry):
+            sweep((G, 0), (G.at[pl.ds(5, 5)], 0), (F, base), (0, 1, 2), 1, CTILES + 1, CLAG)
+            return carry
+
+        lax.fori_loop(0, SUBCYCLES - EARLY, chunk_cycle, 0)
+
+        def finish(n, carry):
+            o = pl.multiple_of(8 * n + CHUNK * i, 8)
+            r = pl.multiple_of(8 * n + 16, 8)
             div = []
             for q in range(3):
-                a = RL[0, q, tile(r + 1), :] - F[W, q, tile(r), :]
-                b = RL[1, q, tile(r), :] - F[Z, q, tile(r + 1), :]
+                a = G[5, q, tile(r + 1), :] - G[W, q, tile(r), :]
+                b = G[6, q, tile(r), :] - G[Z, q, tile(r + 1), :]
                 div.append(a + b)
             div = merged(div)
             w, z, p, m, t = (
-                merged([F[f, q, tile(r), :] for q in range(3)]) for f in (W, Z, PP, MM, TT))
+                merged([G[f, q, tile(r), :] for q in range(3)]) for f in (W, Z, PP, MM, TT))
             for q in range(2):
                 conc = IN[6, q, tile(o), :]
-                OUT[0, q, tile(o), :] = w[q] + z[q]
-                OUT[1, q, tile(o), :] = w[q] - z[q]
-                OUT[2, q, tile(o), :] = (p[q] + m[q]) * (0.5 / BETA)
-                OUT[3, q, tile(o), :] = t[q] * (1.0 / BETA)
-                OUT[4, q, tile(o), :] = (p[q] - m[q]) * (0.25 / BETA)
-                OUT[5, q, tile(o), :] = jnp.clip(conc - conc * div[q], 0.0, 1.0)
-        return carry
-
-    lax.fori_loop(0, ROWS // 16, finish, 0)
-    targets = [vel_o.at[0, 0], vel_o.at[0, 1], st_o.at[0, 0], st_o.at[0, 1], st_o.at[0, 2],
-               conc_o.at[0]]
-    stores = []
-    for n, target in enumerate(targets):
-        for q in range(2):
-            stores.append(pltpu.make_async_copy(
-                OUT.at[n, q], target.at[whole, halves[q]], out_sem.at[2 * n + q]))
-    for copy in stores:
+                FB[0, q, tile(o), :] = jnp.clip(conc - conc * div[q], 0.0, 1.0)
+                FB[1, q, tile(o), :] = w[q] + z[q]
+                FB[2, q, tile(o), :] = w[q] - z[q]
+                OUT[0, q, tile(o), :] = (p[q] + m[q]) * (0.5 / BETA)
+                OUT[1, q, tile(o), :] = t[q] * (1.0 / BETA)
+                OUT[2, q, tile(o), :] = (p[q] - m[q]) * (0.25 / BETA)
+            return carry
+
+        lax.fori_loop(0, CHUNK // 8, finish, 0)
+        for d in (1, 2, 3):
+            wanted, copy = y_copy(i, d)
+            pl.when(wanted)(copy.start)
+        for copy in chunk_stores(i):
+            copy.start()
+        if place:
+            partial(order[place - 1])
+    partial(order[-1])
+
+    z_copy.wait_recv()
+
+    def combine(n, carry):
+        r = pl.multiple_of(8 * n, 8)
+        for f in range(3):
+            for q in range(2):
+                sa, sb = PART[z_hi, 0, f, q, tile(r), :], ZR[0, f, q, tile(r), :]
+                ma, mb = PART[z_hi, 1, f, q, tile(r), :], ZR[1, f, q, tile(r), :]
+                STAT[0, f, q, tile(r), :] = (sa + sb) * 0.125
+                STAT[1, f, q, tile(r), :] = ((ma + mb) + (sa - sb) * (sa - sb) * 0.125) * 0.125
+        return carry
+
+    lax.fori_loop(0, OWN // 8, combine, 0)
+    results = [
+        pltpu.make_async_copy(
+            STAT.at[n, :, q], target.at[:, :, halves[q]], out_sem.at[40 + 2 * n + q])
+        for n, target in enumerate((mean_o, var_o)) for q in range(2)]
+    for copy in results:
         copy.start()
-    for copy in stores:
+    for i in order:
+        for copy in chunk_stores(i):
+            copy.wait()
+        for d in (1, 2, 3):
+            wanted, copy = y_copy(i, d)
+            pl.when(wanted)(copy.wait_send)
+    z_copy.wait_send()
+    for copy in results:
         copy.wait()
 
 
@@ -378,15 +491,17 @@
          ocean_mask, ice_blocks):
     f32 = jnp.float32
     anywhere = pl.BlockSpec(memory_space=pl.ANY)
-    final_vel, final_stress, drifted = pl.pallas_call(
+    stat = jax.ShapeDtypeStruct((3, OWN, 2 * LANES), f32)
+    return pl.pallas_call(
         kernel,
         out_shape=(
             jax.ShapeDtypeStruct(velocity.shape, f32),
             jax.ShapeDtypeStruct(stress.shape, f32),
-            jax.ShapeDtypeStruct(concentration.shape, f32),
+            stat,
+            stat,
         ),
         in_specs=[anywhere] * 8 + [pl.BlockSpec(memory_space=pltpu.SMEM)],
-        out_specs=(anywhere,) * 3,
+        out_specs=(anywhere,) * 4,
         scratch_shapes=[
             pltpu.VMEM((13, 3, ALLOC, LANES), f32),
             pltpu.VMEM((5, 3, ALLOC, LANES), f32),
@@ -394,24 +509,27 @@
             pltpu.VMEM((2, ROWS, LANES), jnp.int32),
             pltpu.VMEM((2, 2, ROWS, LANES), f32),
             pltpu.VMEM((2, 2, ROWS, LANES), f32),
-            pltpu.VMEM((6, 2, ROWS, LANES), f32),
+            pltpu.VMEM((3, 2, ROWS, LANES), f32),
+            pltpu.VMEM((10, 3, 8 * (CTILES + 2), LANES), f32),
+            pltpu.VMEM((3, 2, ROWS, LANES), f32),
+            pltpu.VMEM((2, 3, 3, 2, OWN, LANES), f32),
+            pltpu.VMEM((2, 2, 3, 2, OWN, LANES), f32),
+            pltpu.VMEM((2, 3, 2, OWN, LANES), f32),
+            pltpu.VMEM((2, 3, 2, OWN, LANES), f32),
             pltpu.SemaphoreType.DMA((26,)),
             pltpu.SemaphoreType.DMA((8,)),
             pltpu.SemaphoreType.DMA((8,)),
-            pltpu.SemaphoreType.DMA((12,)),
+            pltpu.SemaphoreType.DMA((44,)),
+            pltpu.SemaphoreType.DMA((6,)),
+            pltpu.SemaphoreType.DMA((6,)),
+            pltpu.SemaphoreType.DMA,
+            pltpu.SemaphoreType.DMA,
         ],
         compiler_params=pltpu.CompilerParams(
             collective_id=0, has_side_effects=True, vmem_limit_bytes=67043328),
         name="ice",
     )(velocity, stress, thickness, concentration, node_mass, wind_stress, ocean_current,
       ocean_mask, ice_blocks)
-    fields = jnp.stack([drifted, final_vel[:, 0], final_vel[:, 1]], axis=1)
-    members = lax.axis_size("ens")
-    gathered = lax.all_to_all(fields, "ens", split_axis=2, concat_axis=0, tiled=True)
-    mean = jnp.sum(gathered, axis=0) / members
-    deviation = gathered - mean[None]
-    spread = jnp.sum(deviation * deviation, axis=0) / members
-    return final_vel, final_stress, mean, spread
 
 
 def solution(mesh):

time: 83.3 us -> 72.3 us (0.87)
  the two profiles are of different devices: /device:TPU:32 before, /device:TPU:61 now
where the time goes in v1:
time: 72.3 us; the launch traced here: 72.1 us
  Pallas kernels  67 us (93%)
  local copies, waits for them, and re-layouts  4.48 us (6%)
    pallas_call x1, Pallas kernels, body(): pl.pallas_call(kernel, out_shape=(jax.ShapeDtypeStruct(velocity.shape, f3...  67 us
    unnamed x10, local copies, waits for them, and re-layouts  4.48 us

profile of v1, /device:TPU:61, one launch (start us, length us, event | category | flops | bytes accessed | tf_op | source)
XLA Modules:
  0.0 72.1 jit_solution(621207122883567079)
XLA Ops:
  0.6 67.0 %ice.1 = (f32[1,2,256,256]{3,2,1,0:T(8,128)}, f32[1,3,256,256]{3,2,1,0:T(8,128)}, f32[3,32,256]{2,1,0:T(8,128)}, f32[3,32,256]{2,1,0:T(8,128)}) custom-call(f32[1,2,256,256]{3,2,1,0:T(8,128)} %vel_h.1, f32[1,3,256,256]{3,2,1,0:T(8,128)} %st_h.1, f32[1,256,256]{2,1,0:T(8,128)} %thick_h.1, f32[1,256,256]{2,1,0:T(8,128)} %conc_h.1, f32[1,256,256]{2,1,0:T(8,128)} %mass_h.1, ...), custom_call_target="tpu_custom_call" | custom-call | tf_op jit(solution)/shard_map/ice/pallas_call | solution.py:495
  67.6 0.0 copy-start
  67.6 1.9 %copy.17 = f32[1,2,256,256]{3,2,1,0:T(8,128)} copy(f32[1,2,256,256]{3,2,1,0:T(8,128)} %get-tuple-element.8) | data formatting | bytes 1048576
  69.5 0.0 copy-done
  69.5 0.0 copy-start.2
  69.5 0.9 %copy.18 = f32[1,3,256,256]{3,2,1,0:T(8,128)} copy(f32[1,3,256,256]{3,2,1,0:T(8,128)S(1)} %copy-done) | data formatting | bytes 1572864
  70.4 0.1 copy-done.2
  70.5 0.0 copy-start.1
  70.5 0.6 copy.19
  71.2 0.3 copy-done.1
  71.4 0.6 copy.20
Async XLA Ops:
  67.6 2.0 %copy-start = (f32[1,3,256,256]{3,2,1,0:T(8,128)S(1)}, f32[1,3,256,256]{3,2,1,0:T(8,128)}, u32[]{:S(2)}) copy-start(f32[1,3,256,256]{3,2,1,0:T(8,128)} %get-tuple-element.9) | copy-start | bytes 2359300
  69.5 1.0 %copy-start.2 = (f32[3,32,256]{2,1,0:T(8,128)S(1)}, f32[3,32,256]{2,1,0:T(8,128)}, u32[]{:S(2)}) copy-start(f32[3,32,256]{2,1,0:T(8,128)} %get-tuple-element.10) | copy-start | bytes 294916
  70.5 0.9 %copy-start.1 = (f32[3,32,256]{2,1,0:T(8,128)S(1)}, f32[3,32,256]{2,1,0:T(8,128)}, u32[]{:S(2)}) copy-start(f32[3,32,256]{2,1,0:T(8,128)} %get-tuple-element.11) | copy-start | bytes 294916

commit v2 on v1

--- a/solution.py
+++ b/solution.py
@@ -23,8 +23,8 @@
 BASE = 24
 HALO = 16
 ALLOC = 312
-FIRST, LAST = 1, 37
-W, Z, PP, MM, TT, SM, MA, WW, WZ, CW, CZ, B2, BB = range(13)
+INNER, INNER_END = 3, 35
+W, Z, PP, MM, TT, SM, MA, WW, WZ, CW, CZ, AC, BB, BS = range(14)
 SENT = 12
 PITCH = 20
 LAG = 8
@@ -45,6 +45,21 @@
 
 
 def sweep(state, rolled, const, tiles, first, last, lag):
+    sweep_many([(state, rolled, const)], tiles, first, last, lag)
+
+
+def sweep_many(regions, tiles, first, last, lag):
+    steps = [updates(*region, tiles) for region in regions]
+    for k in range(last - first + lag):
+        for stress, momentum in steps:
+            if first + k < last:
+                stress(first + k)
+        for stress, momentum in steps:
+            if k >= lag:
+                momentum(first + k - lag)
+
+
+def updates(state, rolled, const, tiles):
     lane = lane_ids()
     low, high = lane == 0, lane == LANES - 1
     (S, so), (RL, ro), (C, co) = state, rolled, const
@@ -99,7 +114,7 @@
             a = mass + drag
             rw = (mass * w + drag * cw) + (fw + const_of(WW, q, r))
             rz = (mass * z + drag * cz) + (fz + const_of(WZ, q, r))
-            root = lax.rsqrt(a * a + const_of(B2, q, r))
+            root = lax.rsqrt(a * a + const_of(BS, q, r))
             quotient = root * root
             a, b = a * quotient, b * quotient
             S[W, q, tile(r + so), :] = a * rw - b * rz
@@ -107,67 +122,60 @@
         for dst, src in ((0, W), (1, Z)):
             turn(dst, src, t, LANES - 1, high)
 
-    for k in range(last - first + lag):
-        if first + k < last:
-            stress(first + k)
-        if k >= lag:
-            momentum(first + k - lag)
+    return stress, momentum
 
 
 def kernel(
     vel_h, st_h, thick_h, conc_h, mass_h, wind_h, cur_h, mask_h, ice_s,
-    vel_o, st_o, mean_o, var_o,
-    F, RL, IN, MK, SP, RP, OUT, G, FB, YR, PART, ZR, STAT,
-    load_sem, send_sem, recv_sem, out_sem, ysend_sem, yrecv_sem, zsend_sem, zrecv_sem,
+    FB, OUT, STAT,
+    F, RL, WG, IN, MK, SP, RP, G, YR, PART, ZR,
+    load_sem, send_sem, recv_sem, ysend_sem, yrecv_sem, zsend_sem, zrecv_sem,
 ):
-    gx, gy = lax.axis_index("gx"), lax.axis_index("gy")
+    gx, gy, ens = lax.axis_index("gx"), lax.axis_index("gy"), lax.axis_index("ens")
     nx, ny = lax.axis_size("gx"), lax.axis_size("gy")
     left, right = lax.rem(gx + nx - 1, nx), lax.rem(gx + 1, nx)
     has_down, has_up = gy > 0, gy < ny - 1
+    z_hi, y = ens // 4, lax.rem(ens, 4)
+    y_peers = [z_hi * 4 + lax.rem(y + d, 4) for d in (1, 2, 3)]
+    partner = (1 - z_hi) * 4 + y
     lane = lane_ids()
-    halves = (pl.ds(0, LANES), pl.ds(LANES, LANES))
-    whole = pl.ds(0, ROWS)
+    zero = jnp.zeros((8, LANES), jnp.float32)
 
     sources = [vel_h.at[0, 0], vel_h.at[0, 1], st_h.at[0, 0], st_h.at[0, 1], st_h.at[0, 2],
                thick_h.at[0], conc_h.at[0], mass_h.at[0], wind_h.at[0, 0], wind_h.at[0, 1],
                cur_h.at[0, 0], cur_h.at[0, 1]]
     loads = []
-    for n, source in enumerate(sources):
-        for q in range(2):
+    for q in range(2):
+        columns = pl.ds(LANES * q, LANES)
+        for n, source in enumerate(sources):
             loads.append(pltpu.make_async_copy(
-                source.at[whole, halves[q]], IN.at[n, q], load_sem.at[2 * n + q]))
-    for q in range(2):
-        loads.append(pltpu.make_async_copy(
-            mask_h.at[whole, halves[q]], MK.at[q], load_sem.at[24 + q]))
+                source.at[:, columns], IN.at[n, q], load_sem.at[2 * n + q]))
+        loads.append(pltpu.make_async_copy(mask_h.at[:, columns], MK.at[q], load_sem.at[24 + q]))
     for copy in loads:
         copy.start()
 
     barrier = pltpu.get_barrier_semaphore()
-    for neighbour in (left, right):
-        pl.semaphore_signal(barrier, inc=1, device_id={"gx": neighbour}, device_id_type=MESH_IDS)
-
-    @pl.when(has_down)
-    def _():
-        pl.semaphore_signal(barrier, inc=1, device_id={"gy": gy - 1}, device_id_type=MESH_IDS)
-
-    @pl.when(has_up)
-    def _():
-        pl.semaphore_signal(barrier, inc=1, device_id={"gy": gy + 1}, device_id_type=MESH_IDS)
-
-    ens = lax.axis_index("ens")
-    z_hi, y = ens // 4, lax.rem(ens, 4)
-    y_peers = [z_hi * 4 + lax.rem(y + d, 4) for d in (1, 2, 3)]
-    partner = (1 - z_hi) * 4 + y
+
+    def greet(**where):
+        pl.semaphore_signal(barrier, inc=1, device_id=where, device_id_type=MESH_IDS)
+
+    greet(gx=left)
+    greet(gx=right)
+    pl.when(has_down)(lambda: greet(gy=gy - 1))
+    pl.when(has_up)(lambda: greet(gy=gy + 1))
     for peer in y_peers + [partner]:
-        pl.semaphore_signal(barrier, inc=1, device_id={"ens": peer}, device_id_type=MESH_IDS)
-
-    zero = jnp.zeros((8, LANES), jnp.float32)
-    for f in (PP, MM, TT):
-        for q in range(3):
-            F[f, q, tile(0), :] = zero
-    for f in (2, 3, 4):
-        for q in range(3):
-            RL[f, q, tile(0), :] = zero
+        greet(ens=peer)
+
+    for q in range(3):
+        for t in (1, 2, INNER_END, INNER_END + 1):
+            for f in range(5):
+                F[f, q, tile(8 * t), :] = zero
+                RL[f, q, tile(8 * t), :] = zero
+        for side in range(2):
+            for f in range(10):
+                WG[side, f, q, tile(0), :] = zero
+        for f in (PP, MM, TT):
+            WG[1, f, q, tile(40), :] = zero
 
     for copy in loads:
         copy.wait()
@@ -215,6 +223,15 @@
 
     lax.fori_loop(0, ROWS // 32, derive, 0)
 
+    def edges(planes):
+        for q in planes:
+            for f in range(5):
+                for t in (3, 4, 5):
+                    WG[0, f, q, tile(8 * t), :] = F[f, q, tile(8 * t), :]
+                for t in (1, 2):
+                    WG[1, f, q, tile(8 * t), :] = F[f, q, tile(8 * t + ROWS), :]
+
+    edges((0, 1))
     pl.semaphore_wait(barrier, 6 + has_down.astype(jnp.int32) + has_up.astype(jnp.int32))
 
     to_left = pltpu.make_async_remote_copy(
@@ -229,20 +246,29 @@
     def row_copies(q, count, n):
         planes = pl.ds(q, count)
 
-        def part(f0, nf, src, dst, rows, slot, row):
+        def state(side, f0, nf, t, tiles, slot, row):
+            rows = pl.ds(8 * t, 8 * tiles)
             return pltpu.make_async_remote_copy(
-                F.at[pl.ds(f0, nf), planes, pl.ds(src, rows)],
-                F.at[pl.ds(f0, nf), planes, pl.ds(dst, rows)],
+                WG.at[side, pl.ds(f0, nf), planes, rows],
+                WG.at[1 - side, pl.ds(f0, nf), planes, rows],
                 send_sem.at[slot], recv_sem.at[slot],
                 device_id={"gy": row}, device_id_type=MESH_IDS)
 
-        down = [part(0, SENT, BASE, BASE + ROWS, HALO, n, gy - 1),
-                part(0, 2, BASE + HALO, BASE + ROWS + HALO, 8, n + 1, gy - 1)]
-        up = [part(0, SENT, BASE + ROWS - HALO, BASE - HALO, HALO, n + 2, gy + 1)]
+        def given(src, dst, slot, row):
+            return pltpu.make_async_remote_copy(
+                F.at[pl.ds(5, SENT - 5), planes, pl.ds(src, HALO)],
+                F.at[pl.ds(5, SENT - 5), planes, pl.ds(dst, HALO)],
+                send_sem.at[slot], recv_sem.at[slot],
+                device_id={"gy": row}, device_id_type=MESH_IDS)
+
+        down = [state(0, 0, 2, 3, 3, n, gy - 1), state(0, 2, 3, 3, 2, n + 1, gy - 1),
+                given(BASE, BASE + ROWS, n + 2, gy - 1)]
+        up = [state(1, 0, 5, 1, 2, n + 3, gy + 1),
+              given(BASE + ROWS - HALO, BASE - HALO, n + 4, gy + 1)]
         return down, up
 
     main_down, main_up = row_copies(0, 2, 2)
-    strip_down, strip_up = row_copies(2, 1, 5)
+    strip_down, strip_up = row_copies(2, 1, 7)
 
     def start_rows(down, up):
         @pl.when(has_down)
@@ -271,98 +297,128 @@
                 copy.wait_recv()
 
     start_rows(main_down, main_up)
+
+    sub = lax.broadcasted_iota(jnp.int32, (8, LANES), 0)
+    grid_rows = ny * ROWS
+
+    def coriolis(t, planes):
+        r = 8 * t if isinstance(t, int) else pl.multiple_of(8 * t, 8)
+        row = (sub + (gy * ROWS - BASE + r)).astype(jnp.float32) + 0.5
+        half = row * (0.5 / grid_rows)
+        for q in planes:
+            b = half * F[MA, q, tile(r), :]
+            F[BB, q, tile(r), :] = b
+            F[BS, q, tile(r), :] = jnp.where(F[AC, q, tile(r), :] > 0.5, b * b, jnp.inf)
+
+    def first_turn(t, planes):
+        r = pl.multiple_of(8 * t, 8)
+        for dst, f in ((0, W), (1, Z)):
+            v = [pltpu.roll(F[f, q, tile(r), :], LANES - 1, 1) for q in planes]
+            if len(v) == 2:
+                v = [jnp.where(lane == LANES - 1, v[1 - n], v[n]) for n in range(2)]
+            for q, value in zip(planes, v):
+                RL[dst, q, tile(r), :] = value
+
+    def ready(planes):
+        def body(n, carry):
+            for k in range(8):
+                coriolis(INNER + 8 * n + k, planes)
+                first_turn(INNER + 8 * n + k, planes)
+            return carry
+
+        lax.fori_loop(0, (INNER_END - INNER) // 8, body, 0)
+
+    whole_state, whole_rolled, const = (F, 0), (RL, 0), (F, 0)
+
+    def inner_cycles(planes):
+        def cycle(n, carry):
+            sweep(whole_state, whole_rolled, const, planes, INNER, INNER_END, LAG)
+            return carry
+
+        lax.fori_loop(0, EARLY, cycle, 0)
+
+    ready((0, 1))
+    def build(block, carry):
+        for n in range(4):
+            r = pl.multiple_of(block * 32 + 8 * n, 8)
+            for f in range(SENT):
+                high = pltpu.roll(F[f, 1, tile(r + BASE), :], 95, 1)
+                F[f, 2, tile(r + BASE), :] = jnp.where(
+                    lane < 48, F[f, 0, tile(r + BASE), :], high)
+        return carry
+
+    lax.fori_loop(0, ROWS // 32, build, 0)
+    inner_cycles((0, 1))
+
     to_left.wait_recv()
     to_right.wait_recv()
 
-    def build(block, carry):
-        for n in range(2):
-            r = pl.multiple_of(block * 16 + 8 * n, 8)
+    def fill(block, carry):
+        for n in range(4):
+            r = pl.multiple_of(block * 32 + 8 * n, 8)
             for part in range(2):
                 from_right, from_left = RP[0, part, tile(r), :], RP[1, part, tile(r), :]
                 for s in range(6):
                     f = 6 * part + s
                     both = jnp.where(slot_mask(PITCH * s + 17, 16), from_left, from_right)
                     both = pltpu.roll(both, (95 - PITCH * s) % LANES, 1)
-                    high = pltpu.roll(F[f, 1, tile(r + BASE), :], 95, 1)
                     F[f, 2, tile(r + BASE), :] = jnp.where(
-                        lane < 48, F[f, 0, tile(r + BASE), :], jnp.where(lane < 95, high, both))
+                        lane < 95, F[f, 2, tile(r + BASE), :], both)
         return carry
 
-    lax.fori_loop(0, ROWS // 16, build, 0)
+    lax.fori_loop(0, ROWS // 32, fill, 0)
+    edges((2,))
     start_rows(strip_down, strip_up)
-
-    def outside(start, count):
-        for f in range(SENT):
-            value = jnp.ones((8, LANES), jnp.float32) if f == MA else zero
-            for q in range(3):
-                for n in range(count):
-                    F[f, q, tile(start + 8 * n), :] = value
-
-    @pl.when(jnp.logical_not(has_down))
-    def _():
-        outside(BASE - HALO, 2)
-
-    @pl.when(jnp.logical_not(has_up))
-    def _():
-        outside(BASE + ROWS, 3)
+    ready((2,))
+    inner_cycles((2,))
 
     to_left.wait_send()
     to_right.wait_send()
     wait_rows(main_down, main_up)
     wait_rows(strip_down, strip_up)
 
-    sub = lax.broadcasted_iota(jnp.int32, (8, LANES), 0)
-    grid_rows = ny * ROWS
-
-    def prepare(t, carry):
-        r = pl.multiple_of(8 * t, 8)
-        row = (sub + (gy * ROWS - BASE + r)).astype(jnp.float32) + 0.5
-        half = row * (0.5 / grid_rows)
+    def outside(side, tiles):
         for q in range(3):
-            b = half * F[MA, q, tile(r), :]
-            F[BB, q, tile(r), :] = b
-            F[B2, q, tile(r), :] = jnp.where(F[B2, q, tile(r), :] > 0.5, b * b, jnp.inf)
+            for t in tiles:
+                for f in range(5):
+                    WG[side, f, q, tile(8 * t), :] = zero
+                if t < 5:
+                    for f in range(5, SENT):
+                        F[f, q, tile(8 * t + ROWS * side), :] = (
+                            jnp.ones((8, LANES), jnp.float32) if f == MA else zero)
+
+    pl.when(jnp.logical_not(has_down))(lambda: outside(0, (1, 2)))
+    pl.when(jnp.logical_not(has_up))(lambda: outside(1, (3, 4, 5)))
+    for t in (1, 2, INNER_END, INNER_END + 1):
+        coriolis(t, (0, 1, 2))
+
+    for side in range(2):
+        for t in (1, 2, 3, 4, 5):
+            for dst, f in ((5, W), (6, Z)):
+                v = [pltpu.roll(WG[side, f, q, tile(8 * t), :], LANES - 1, 1) for q in range(3)]
+                v[:2] = [jnp.where(lane == LANES - 1, v[1 - n], v[n]) for n in range(2)]
+                for q in range(3):
+                    WG[side, dst, q, tile(8 * t), :] = v[q]
+
+    def wedge_cycle(n, carry):
+        sweep_many(
+            [((WG.at[side, pl.ds(0, 5)], 0), (WG.at[side, pl.ds(5, 5)], 0), (F, ROWS * side))
+             for side in range(2)], (0, 1, 2), 1, 5, 2)
         return carry
 
-    lax.fori_loop(FIRST, LAST, prepare, 0)
-
-    def turn_first(t, carry):
-        r = pl.multiple_of(8 * t, 8)
-        for dst, f in ((0, W), (1, Z)):
-            v = [pltpu.roll(F[f, q, tile(r), :], LANES - 1, 1) for q in range(3)]
-            RL[dst, 0, tile(r), :] = jnp.where(lane == LANES - 1, v[1], v[0])
-            RL[dst, 1, tile(r), :] = jnp.where(lane == LANES - 1, v[0], v[1])
-            RL[dst, 2, tile(r), :] = v[2]
-        return carry
-
-    lax.fori_loop(FIRST, LAST + 1, turn_first, 0)
-
-    whole_state, whole_rolled, const = (F, 0), (RL, 0), (F, 0)
-
-    def main_cycle(n, carry):
-        sweep(whole_state, whole_rolled, const, (0, 1), FIRST, LAST, LAG)
-        return carry
-
-    def strip_cycle(n, carry):
-        sweep(whole_state, whole_rolled, const, (2,), FIRST, LAST, LAG)
-        return carry
-
-    lax.fori_loop(0, EARLY, main_cycle, 0)
-    lax.fori_loop(0, EARLY, strip_cycle, 0)
+    lax.fori_loop(0, EARLY, wedge_cycle, 0)
+    for side, tiles in ((0, (2, 3)), (1, (2, 3, 4))):
+        for t in tiles:
+            for q in range(3):
+                for f in range(5):
+                    F[f, q, tile(8 * t + ROWS * side), :] = WG[side, f, q, tile(8 * t), :]
+                    if f < 2:
+                        RL[f, q, tile(8 * t + ROWS * side), :] = WG[side, 5 + f, q, tile(8 * t), :]
 
     def merged(values):
         low = jnp.where(lane < 16, values[2], values[0])
         high = jnp.where(lane >= 108, pltpu.roll(values[2], 33, 1), values[1])
         return low, high
-
-    def chunk_stores(i):
-        rows = pl.ds(CHUNK * i, CHUNK)
-        targets = [(FB.at[1], vel_o.at[0, 0]), (FB.at[2], vel_o.at[0, 1]), (OUT.at[0], st_o.at[0, 0]),
-                   (OUT.at[1], st_o.at[0, 1]), (OUT.at[2], st_o.at[0, 2])]
-        return [
-            pltpu.make_async_copy(
-                source.at[q, rows], target.at[rows, halves[q]], out_sem.at[10 * i + 2 * n + q])
-            for n, (source, target) in enumerate(targets) for q in range(2)]
 
     def y_copy(i, d):
         target = lax.rem(y + d, 4)
@@ -401,10 +457,7 @@
                 return carry
 
             lax.fori_loop(0, OWN // 8, reduce, 0)
-
-            @pl.when(z_hi != block)
-            def _():
-                z_copy.start()
+            pl.when(z_hi != block)(z_copy.start)
 
     order = (0, 2, 1, 3)
     for place, i in enumerate(order):
@@ -421,14 +474,14 @@
         lax.fori_loop(0, CTILES + 2, fetch, 0)
 
         def chunk_cycle(n, carry):
-            sweep((G, 0), (G.at[pl.ds(5, 5)], 0), (F, base), (0, 1, 2), 1, CTILES + 1, CLAG)
+            sweep((G.at[pl.ds(0, 5)], 0), (G.at[pl.ds(5, 5)], 0), (F, base), (0, 1, 2), 1,
+                  CTILES + 1, CLAG)
             return carry
 
         lax.fori_loop(0, SUBCYCLES - EARLY, chunk_cycle, 0)
 
-        def finish(n, carry):
-            o = pl.multiple_of(8 * n + CHUNK * i, 8)
-            r = pl.multiple_of(8 * n + 16, 8)
+        for n in range(CHUNK // 8):
+            o, r = 8 * n + CHUNK * i, 8 * n + 16
             div = []
             for q in range(3):
                 a = G[5, q, tile(r + 1), :] - G[W, q, tile(r), :]
@@ -445,91 +498,101 @@
                 OUT[0, q, tile(o), :] = (p[q] + m[q]) * (0.5 / BETA)
                 OUT[1, q, tile(o), :] = t[q] * (1.0 / BETA)
                 OUT[2, q, tile(o), :] = (p[q] - m[q]) * (0.25 / BETA)
-            return carry
-
-        lax.fori_loop(0, CHUNK // 8, finish, 0)
         for d in (1, 2, 3):
             wanted, copy = y_copy(i, d)
             pl.when(wanted)(copy.start)
-        for copy in chunk_stores(i):
-            copy.start()
         if place:
             partial(order[place - 1])
     partial(order[-1])
 
     z_copy.wait_recv()
-
-    def combine(n, carry):
-        r = pl.multiple_of(8 * n, 8)
+    for n in range(OWN // 8):
+        r = 8 * n
         for f in range(3):
             for q in range(2):
                 sa, sb = PART[z_hi, 0, f, q, tile(r), :], ZR[0, f, q, tile(r), :]
                 ma, mb = PART[z_hi, 1, f, q, tile(r), :], ZR[1, f, q, tile(r), :]
                 STAT[0, f, q, tile(r), :] = (sa + sb) * 0.125
                 STAT[1, f, q, tile(r), :] = ((ma + mb) + (sa - sb) * (sa - sb) * 0.125) * 0.125
-        return carry
-
-    lax.fori_loop(0, OWN // 8, combine, 0)
-    results = [
-        pltpu.make_async_copy(
-            STAT.at[n, :, q], target.at[:, :, halves[q]], out_sem.at[40 + 2 * n + q])
-        for n, target in enumerate((mean_o, var_o)) for q in range(2)]
-    for copy in results:
-        copy.start()
     for i in order:
-        for copy in chunk_stores(i):
-            copy.wait()
         for d in (1, 2, 3):
             wanted, copy = y_copy(i, d)
             pl.when(wanted)(copy.wait_send)
     z_copy.wait_send()
-    for copy in results:
+
+
+def emit(FB, OUT, STAT, vel_o, st_o, mean_o, var_o, sem):
+    copies = []
+    for q in range(2):
+        columns = pl.ds(LANES * q, LANES)
+        pairs = [(OUT.at[n, q], st_o.at[0, n]) for n in range(3)]
+        pairs += [(FB.at[1 + n, q], vel_o.at[0, n]) for n in range(2)]
+        for source, target in pairs:
+            copies.append((source, target.at[:, columns]))
+        for n, target in enumerate((mean_o, var_o)):
+            copies.append((STAT.at[n, :, q], target.at[:, :, columns]))
+    copies = [pltpu.make_async_copy(a, b, sem.at[n]) for n, (a, b) in enumerate(copies)]
+    for copy in copies:
+        copy.start()
+    for copy in copies:
         copy.wait()
 
 
 def body(velocity, stress, thickness, concentration, node_mass, wind_stress, ocean_current,
          ocean_mask, ice_blocks):
     f32 = jnp.float32
-    anywhere = pl.BlockSpec(memory_space=pl.ANY)
+    hbm = pl.BlockSpec(memory_space=pltpu.HBM)
+    vmem = pl.BlockSpec(memory_space=pltpu.VMEM)
     stat = jax.ShapeDtypeStruct((3, OWN, 2 * LANES), f32)
+    big = [pltpu.with_memory_space_constraint(x, pltpu.HBM) for x in (velocity, stress, thickness, concentration, node_mass, wind_stress, ocean_current, ocean_mask)]
+    results = pl.pallas_call(
+        kernel,
+        out_shape=(
+            jax.ShapeDtypeStruct((3, 2, ROWS, LANES), f32),
+            jax.ShapeDtypeStruct((3, 2, ROWS, LANES), f32),
+            jax.ShapeDtypeStruct((2, 3, 2, OWN, LANES), f32),
+        ),
+        in_specs=[hbm] * 8 + [pl.BlockSpec(memory_space=pltpu.SMEM)],
+        out_specs=(vmem,) * 3,
+        scratch_shapes=[
+            pltpu.VMEM((14, 3, ALLOC, LANES), f32),
+            pltpu.VMEM((5, 3, ALLOC, LANES), f32),
+            pltpu.VMEM((2, 10, 3, 48, LANES), f32),
+            pltpu.VMEM((12, 2, ROWS, LANES), f32),
+            pltpu.VMEM((2, ROWS, LANES), jnp.int32),
+            pltpu.VMEM((2, 2, ROWS, LANES), f32),
+            pltpu.VMEM((2, 2, ROWS, LANES), f32),
+            pltpu.VMEM((10, 3, 8 * (CTILES + 2), LANES), f32),
+            pltpu.VMEM((2, 3, 3, 2, OWN, LANES), f32),
+            pltpu.VMEM((2, 2, 3, 2, OWN, LANES), f32),
+            pltpu.VMEM((2, 3, 2, OWN, LANES), f32),
+            pltpu.SemaphoreType.DMA((26,)),
+            pltpu.SemaphoreType.DMA((12,)),
+            pltpu.SemaphoreType.DMA((12,)),
+            pltpu.SemaphoreType.DMA((6,)),
+            pltpu.SemaphoreType.DMA((6,)),
+            pltpu.SemaphoreType.DMA,
+            pltpu.SemaphoreType.DMA,
+        ],
+        compiler_params=pltpu.CompilerParams(
+            collective_id=0, has_side_effects=True, vmem_limit_bytes=40 * 1024 * 1024),
+        name="ice",
+    )(*big,
+      ice_blocks)
     return pl.pallas_call(
-        kernel,
+        emit,
         out_shape=(
             jax.ShapeDtypeStruct(velocity.shape, f32),
             jax.ShapeDtypeStruct(stress.shape, f32),
             stat,
             stat,
         ),
-        in_specs=[anywhere] * 8 + [pl.BlockSpec(memory_space=pltpu.SMEM)],
-        out_specs=(anywhere,) * 4,
-        scratch_shapes=[
-            pltpu.VMEM((13, 3, ALLOC, LANES), f32),
-            pltpu.VMEM((5, 3, ALLOC, LANES), f32),
-            pltpu.VMEM((12, 2, ROWS, LANES), f32),
-            pltpu.VMEM((2, ROWS, LANES), jnp.int32),
-            pltpu.VMEM((2, 2, ROWS, LANES), f32),
-            pltpu.VMEM((2, 2, ROWS, LANES), f32),
-            pltpu.VMEM((3, 2, ROWS, LANES), f32),
-            pltpu.VMEM((10, 3, 8 * (CTILES + 2), LANES), f32),
-            pltpu.VMEM((3, 2, ROWS, LANES), f32),
-            pltpu.VMEM((2, 3, 3, 2, OWN, LANES), f32),
-            pltpu.VMEM((2, 2, 3, 2, OWN, LANES), f32),
-            pltpu.VMEM((2, 3, 2, OWN, LANES), f32),
-            pltpu.VMEM((2, 3, 2, OWN, LANES), f32),
-            pltpu.SemaphoreType.DMA((26,)),
-            pltpu.SemaphoreType.DMA((8,)),
-            pltpu.SemaphoreType.DMA((8,)),
-            pltpu.SemaphoreType.DMA((44,)),
-            pltpu.SemaphoreType.DMA((6,)),
-            pltpu.SemaphoreType.DMA((6,)),
-            pltpu.SemaphoreType.DMA,
-            pltpu.SemaphoreType.DMA,
-        ],
-        compiler_params=pltpu.CompilerParams(
-            collective_id=0, has_side_effects=True, vmem_limit_bytes=67043328),
-        name="ice",
-    )(velocity, stress, thickness, concentration, node_mass, wind_stress, ocean_current,
-      ocean_mask, ice_blocks)
+        in_specs=[vmem] * 3,
+        out_specs=(hbm,) * 4,
+        scratch_shapes=[pltpu.SemaphoreType.DMA((14,))],
+        compiler_params=pltpu.CompilerParams(vmem_limit_bytes=8 * 1024 * 1024),
+        name="emit",
+    )(*results)
 
 
 def solution(mesh):

time: 72.3 us -> 59 us (0.82)
  the two profiles are of different devices: /device:TPU:61 before, /device:TPU:16 now
where the time goes in v2:
time: 59 us; the launch traced here: 58.9 us
  Pallas kernels  57.6 us (98%)
  local copies, waits for them, and re-layouts  0.68 us (1%)
  between operations  0.65 us (1%)
    pallas_call x1, Pallas kernels, body(): pl.pallas_call(kernel, out_shape=(jax.ShapeDtypeStruct((3, 2, ROWS, LANES...  56.3 us
    pallas_call x1, Pallas kernels, body(): pl.pallas_call(emit, out_shape=(jax.ShapeDtypeStruct(velocity.shape, f32)...  1.22 us

profile of v2, /device:TPU:16, one launch (start us, length us, event | category | flops | bytes accessed | tf_op | source)
XLA Modules:
  0.0 58.9 jit_solution(8479797855120698505)
XLA Ops:
  0.6 0.0 copy-start
  0.6 0.7 %copy-done = s32[1,8,8]{2,1,0:T(8,128)S(1)} copy-done((s32[1,8,8]{2,1,0:T(8,128)S(1)}, s32[1,8,8]{2,1,0:T(8,128)}, u32[]{:S(2)}) %copy-start) | copy-done | bytes 280
  1.3 56.3 %ice.1 = (f32[3,2,256,128]{3,2,1,0:T(8,128)S(1)}, f32[3,2,256,128]{3,2,1,0:T(8,128)S(1)}, f32[2,3,2,32,128]{4,3,2,1,0:T(8,128)S(1)}) custom-call(f32[1,2,256,256]{3,2,1,0:T(8,128)} %vel_h.1, f32[1,3,256,256]{3,2,1,0:T(8,128)} %st_h.1, f32[1,256,256]{2,1,0:T(8,128)} %thick_h.1, f32[1,256,256]{2,1,0:T(8,128)} %conc_h.1, f32[1,256,256]{2,1,0:T(8,128)} %mass_h.1, ...), custom_call_target="tpu_custom_call" | custom-call | tf_op jit(solution)/shard_map/ice/pallas_call | solution.py:548
  57.7 1.2 %emit.1 = (f32[1,2,256,256]{3,2,1,0:T(8,128)}, f32[1,3,256,256]{3,2,1,0:T(8,128)}, f32[3,32,256]{2,1,0:T(8,128)}, f32[3,32,256]{2,1,0:T(8,128)}) custom-call(f32[3,2,256,128]{3,2,1,0:T(8,128)S(1)} %get-tuple-element.7.FB, f32[3,2,256,128]{3,2,1,0:T(8,128)S(1)} %get-tuple-element.8.OUT, f32[2,3,2,32,128]{4,3,2,1,0:T(8,128)S(1)} %get-tuple-element.9.STAT), custom_call_target="tpu_custom_call" | custom-call | tf_op jit(solution)/shard_map/emit/pallas_call | solution.py:582
Async XLA Ops:
  0.6 0.7 %copy-start = (s32[1,8,8]{2,1,0:T(8,128)S(1)}, s32[1,8,8]{2,1,0:T(8,128)}, u32[]{:S(2)}) copy-start(s32[1,8,8]{2,1,0:T(8,128)} %ice_s.1) | copy-start | bytes 772

commit v3 on v2

--- a/solution.py
+++ b/solution.py
@@ -29,8 +29,7 @@
 PITCH = 20
 LAG = 8
 EARLY = 8
-CHUNK = 64
-CTILES = CHUNK // 8 + 2
+GROWS = 12
 CLAG = 3
 OWN = 32
 MESH_IDS = pl.DeviceIdType.MESH
@@ -126,10 +125,10 @@
 
 
 def kernel(
-    vel_h, st_h, thick_h, conc_h, mass_h, wind_h, cur_h, mask_h, ice_s,
+    vel_h, st_h, thick_h, conc_h, mass_h, wind_h, cur_h, mask_h, ice_h,
     FB, OUT, STAT,
-    F, RL, WG, IN, MK, SP, RP, G, YR, PART, ZR,
-    load_sem, send_sem, recv_sem, ysend_sem, yrecv_sem, zsend_sem, zrecv_sem,
+    F, RL, WG, IN, MK, SP, RP, G, YR, PART, ZR, ice_s,
+    load_sem, ice_sem, send_sem, recv_sem, ysend_sem, yrecv_sem, zsend_sem, zrecv_sem,
 ):
     gx, gy, ens = lax.axis_index("gx"), lax.axis_index("gy"), lax.axis_index("ens")
     nx, ny = lax.axis_size("gx"), lax.axis_size("gy")
@@ -137,21 +136,24 @@
     has_down, has_up = gy > 0, gy < ny - 1
     z_hi, y = ens // 4, lax.rem(ens, 4)
     y_peers = [z_hi * 4 + lax.rem(y + d, 4) for d in (1, 2, 3)]
-    partner = (1 - z_hi) * 4 + y
     lane = lane_ids()
     zero = jnp.zeros((8, LANES), jnp.float32)
 
     sources = [vel_h.at[0, 0], vel_h.at[0, 1], st_h.at[0, 0], st_h.at[0, 1], st_h.at[0, 2],
                thick_h.at[0], conc_h.at[0], mass_h.at[0], wind_h.at[0, 0], wind_h.at[0, 1],
                cur_h.at[0, 0], cur_h.at[0, 1]]
-    loads = []
-    for q in range(2):
-        columns = pl.ds(LANES * q, LANES)
-        for n, source in enumerate(sources):
-            loads.append(pltpu.make_async_copy(
-                source.at[:, columns], IN.at[n, q], load_sem.at[2 * n + q]))
-        loads.append(pltpu.make_async_copy(mask_h.at[:, columns], MK.at[q], load_sem.at[24 + q]))
-    for copy in loads:
+    ice_load = pltpu.make_async_copy(ice_h, ice_s, ice_sem)
+    ice_load.start()
+    loads = [[], []]
+    for half in range(2):
+        rows = pl.ds(ROWS // 2 * half, ROWS // 2)
+        for q in range(2):
+            columns = pl.ds(LANES * q, LANES)
+            places = [IN.at[n, q, rows] for n in range(12)] + [MK.at[q, rows]]
+            for n, (source, place) in enumerate(zip(sources + [mask_h], places)):
+                loads[half].append(pltpu.make_async_copy(
+                    source.at[rows, columns], place, load_sem.at[26 * half + 13 * q + n]))
+    for copy in loads[0] + loads[1]:
         copy.start()
 
     barrier = pltpu.get_barrier_semaphore()
@@ -163,8 +165,8 @@
     greet(gx=right)
     pl.when(has_down)(lambda: greet(gy=gy - 1))
     pl.when(has_up)(lambda: greet(gy=gy + 1))
-    for peer in y_peers + [partner]:
-        greet(ens=peer)
+    for d in range(1, 8):
+        greet(ens=lax.rem(ens + d, 8))
 
     for q in range(3):
         for t in (1, 2, INNER_END, INNER_END + 1):
@@ -176,9 +178,6 @@
                 WG[side, f, q, tile(0), :] = zero
         for f in (PP, MM, TT):
             WG[1, f, q, tile(40), :] = zero
-
-    for copy in loads:
-        copy.wait()
 
     def slot_mask(start, width):
         return lax.rem(lane - start + 2 * LANES, LANES) < width
@@ -221,7 +220,11 @@
                 SP[1, part, tile(r), :] = to_right
         return carry
 
-    lax.fori_loop(0, ROWS // 32, derive, 0)
+    ice_load.wait()
+    for half in range(2):
+        for copy in loads[half]:
+            copy.wait()
+        lax.fori_loop(4 * half, 4 * half + 4, derive, 0)
 
     def edges(planes):
         for q in planes:
@@ -232,7 +235,7 @@
                     WG[1, f, q, tile(8 * t), :] = F[f, q, tile(8 * t + ROWS), :]
 
     edges((0, 1))
-    pl.semaphore_wait(barrier, 6 + has_down.astype(jnp.int32) + has_up.astype(jnp.int32))
+    pl.semaphore_wait(barrier, 9 + has_down.astype(jnp.int32) + has_up.astype(jnp.int32))
 
     to_left = pltpu.make_async_remote_copy(
         SP.at[0], RP.at[0], send_sem.at[0], recv_sem.at[0],
@@ -420,105 +423,108 @@
         high = jnp.where(lane >= 108, pltpu.roll(values[2], 33, 1), values[1])
         return low, high
 
-    def y_copy(i, d):
-        target = lax.rem(y + d, 4)
-        block = i // 2
-        rows = pl.ds(pl.multiple_of(CHUNK * i + OWN * lax.rem(target, 2), 8), OWN)
-        return target // 2 == i % 2, pltpu.make_async_remote_copy(
-            FB.at[:, :, rows], YR.at[block, 3 - d],
-            ysend_sem.at[3 * block + d - 1], yrecv_sem.at[3 * block + 3 - d],
-            device_id={"ens": y_peers[d - 1]}, device_id_type=MESH_IDS)
-
-    z_copy = pltpu.make_async_remote_copy(
-        PART.at[1 - z_hi], ZR, zsend_sem, zrecv_sem,
-        device_id={"ens": partner}, device_id_type=MESH_IDS)
-
-    def partial(i):
-        block = i // 2
-
-        @pl.when(y // 2 == i % 2)
-        def _():
+    def y_copy(e, d):
+        rows = pl.ds(pl.multiple_of(OWN * e + 8 * lax.rem(y + d, 4), 8), 8)
+        return pltpu.make_async_remote_copy(
+            FB.at[:, :, rows], YR.at[e, 3 - d], ysend_sem.at[3 * e + d - 1],
+            yrecv_sem.at[3 * e + 3 - d], device_id={"ens": y_peers[d - 1]},
+            device_id_type=MESH_IDS)
+
+    def z_copy(e):
+        return pltpu.make_async_remote_copy(
+            PART.at[e], ZR.at[ens], zsend_sem.at[e], zrecv_sem.at[ens],
+            device_id={"ens": jnp.int32(e)}, device_id_type=MESH_IDS)
+
+    def from_member(d):
+        sender = lax.rem(ens + d, 8)
+        return pltpu.make_async_remote_copy(
+            PART.at[0], ZR.at[sender], zsend_sem.at[0], zrecv_sem.at[sender],
+            device_id={"ens": sender}, device_id_type=MESH_IDS)
+
+    def partial(blocks):
+        for e in blocks:
             for d in (1, 2, 3):
-                y_copy(i, d)[1].wait_recv()
-            own = CHUNK * i + OWN * lax.rem(y, 2)
-
-            def reduce(n, carry):
-                r = pl.multiple_of(8 * n, 8)
-                for f in range(3):
-                    for q in range(2):
-                        v = [YR[block, d, f, q, tile(r), :] for d in range(3)]
-                        v.append(FB[f, q, tile(pl.multiple_of(own + r, 8)), :])
-                        total = (v[0] + v[1]) + (v[2] + v[3])
-                        mean = total * 0.25
-                        e = [x - mean for x in v]
-                        PART[block, 0, f, q, tile(r), :] = total
-                        PART[block, 1, f, q, tile(r), :] = (
-                            (e[0] * e[0] + e[1] * e[1]) + (e[2] * e[2] + e[3] * e[3]))
-                return carry
-
-            lax.fori_loop(0, OWN // 8, reduce, 0)
-            pl.when(z_hi != block)(z_copy.start)
-
-    order = (0, 2, 1, 3)
-    for place, i in enumerate(order):
-        base = BASE - 16 + CHUNK * i
-
-        def fetch(t, carry):
-            r = pl.multiple_of(8 * t, 8)
-            for q in range(3):
-                for f in range(5):
-                    G[f, q, tile(r), :] = F[f, q, tile(r + base), :]
-                    G[5 + f, q, tile(r), :] = RL[f, q, tile(r + base), :]
+                y_copy(e, d).wait_recv()
+            own = pl.ds(pl.multiple_of(OWN * e + 8 * y, 8), 8)
+            for f in range(3):
+                for q in range(2):
+                    v = [YR[e, n, f, q] for n in range(3)] + [FB[f, q, own, :]]
+                    total = (v[0] + v[1]) + (v[2] + v[3])
+                    mean = total * 0.25
+                    x = [value - mean for value in v]
+                    PART[e, 0, f, q] = total
+                    PART[e, 1, f, q] = (x[0] * x[0] + x[1] * x[1]) + (x[2] * x[2] + x[3] * x[3])
+            pl.when(ens != e)(z_copy(e).start)
+
+    def chunk(pieces, split, earlier):
+        regions = []
+        for n, (e, count) in enumerate(pieces):
+            base = BASE - 16 + OWN * e
+            top = 8 * GROWS * n
+            for t in range(4 * count + 4):
+                for q in range(3):
+                    for f in range(5):
+                        G[f, q, tile(8 * t + top), :] = F[f, q, tile(8 * t + base), :]
+                        G[5 + f, q, tile(8 * t + top), :] = RL[f, q, tile(8 * t + base), :]
+            regions.append(((G.at[pl.ds(0, 5)], top), (G.at[pl.ds(5, 5)], top), (F, base)))
+        last = 4 * pieces[0][1] + 3
+
+        def cycle(n, carry):
+            sweep_many(regions, (0, 1, 2), 1, last, CLAG)
+            if earlier:
+                pl.when(n == split)(lambda: partial(earlier))
             return carry
 
-        lax.fori_loop(0, CTILES + 2, fetch, 0)
-
-        def chunk_cycle(n, carry):
-            sweep((G.at[pl.ds(0, 5)], 0), (G.at[pl.ds(5, 5)], 0), (F, base), (0, 1, 2), 1,
-                  CTILES + 1, CLAG)
-            return carry
-
-        lax.fori_loop(0, SUBCYCLES - EARLY, chunk_cycle, 0)
-
-        for n in range(CHUNK // 8):
-            o, r = 8 * n + CHUNK * i, 8 * n + 16
-            div = []
-            for q in range(3):
-                a = G[5, q, tile(r + 1), :] - G[W, q, tile(r), :]
-                b = G[6, q, tile(r), :] - G[Z, q, tile(r + 1), :]
-                div.append(a + b)
-            div = merged(div)
-            w, z, p, m, t = (
-                merged([G[f, q, tile(r), :] for q in range(3)]) for f in (W, Z, PP, MM, TT))
-            for q in range(2):
-                conc = IN[6, q, tile(o), :]
-                FB[0, q, tile(o), :] = jnp.clip(conc - conc * div[q], 0.0, 1.0)
-                FB[1, q, tile(o), :] = w[q] + z[q]
-                FB[2, q, tile(o), :] = w[q] - z[q]
-                OUT[0, q, tile(o), :] = (p[q] + m[q]) * (0.5 / BETA)
-                OUT[1, q, tile(o), :] = t[q] * (1.0 / BETA)
-                OUT[2, q, tile(o), :] = (p[q] - m[q]) * (0.25 / BETA)
-        for d in (1, 2, 3):
-            wanted, copy = y_copy(i, d)
-            pl.when(wanted)(copy.start)
-        if place:
-            partial(order[place - 1])
-    partial(order[-1])
-
-    z_copy.wait_recv()
-    for n in range(OWN // 8):
-        r = 8 * n
+        lax.fori_loop(0, SUBCYCLES - EARLY, cycle, 0)
+
+        for n, (e, count) in enumerate(pieces):
+            for k in range(4 * count):
+                o, r = OWN * e + 8 * k, 8 * GROWS * n + 8 * k + 16
+                div = []
+                for q in range(3):
+                    a = G[5, q, tile(r + 1), :] - G[W, q, tile(r), :]
+                    b = G[6, q, tile(r), :] - G[Z, q, tile(r + 1), :]
+                    div.append(a + b)
+                div = merged(div)
+                w, z, p, m, t = (
+                    merged([G[f, q, tile(r), :] for q in range(3)]) for f in (W, Z, PP, MM, TT))
+                for q in range(2):
+                    conc = IN[6, q, tile(o), :]
+                    FB[0, q, tile(o), :] = jnp.clip(conc - conc * div[q], 0.0, 1.0)
+                    FB[1, q, tile(o), :] = w[q] + z[q]
+                    FB[2, q, tile(o), :] = w[q] - z[q]
+                    OUT[0, q, tile(o), :] = (p[q] + m[q]) * (0.5 / BETA)
+                    OUT[1, q, tile(o), :] = t[q] * (1.0 / BETA)
+                    OUT[2, q, tile(o), :] = (p[q] - m[q]) * (0.25 / BETA)
+            for block in range(e, e + count):
+                for d in (1, 2, 3):
+                    y_copy(block, d).start()
+
+    chunk([(0, 2)], 0, ())
+    chunk([(6, 2)], 0, ())
+    chunk([(2, 1), (5, 1)], 3, (0, 1))
+    chunk([(3, 2)], 4, (6, 7))
+    partial((2, 5))
+    partial((3, 4))
+
+    for f in range(3):
+        for q in range(2):
+            for n in range(2):
+                ZR[ens, n, f, q] = PART[ens, n, f, q]
+    for d in range(1, 8):
+        from_member(d).wait_recv()
+    for k in range(4):
+        rows = tile(8 * k)
         for f in range(3):
             for q in range(2):
-                sa, sb = PART[z_hi, 0, f, q, tile(r), :], ZR[0, f, q, tile(r), :]
-                ma, mb = PART[z_hi, 1, f, q, tile(r), :], ZR[1, f, q, tile(r), :]
-                STAT[0, f, q, tile(r), :] = (sa + sb) * 0.125
-                STAT[1, f, q, tile(r), :] = ((ma + mb) + (sa - sb) * (sa - sb) * 0.125) * 0.125
-    for i in order:
+                sa, sb = ZR[k, 0, f, q], ZR[4 + k, 0, f, q]
+                ma, mb = ZR[k, 1, f, q], ZR[4 + k, 1, f, q]
+                STAT[0, f, q, rows, :] = (sa + sb) * 0.125
+                STAT[1, f, q, rows, :] = ((ma + mb) + (sa - sb) * (sa - sb) * 0.125) * 0.125
+    for e in range(8):
         for d in (1, 2, 3):
-            wanted, copy = y_copy(i, d)
-            pl.when(wanted)(copy.wait_send)
-    z_copy.wait_send()
+            y_copy(e, d).wait_send()
+        pl.when(ens != e)(z_copy(e).wait_send)
 
 
 def emit(FB, OUT, STAT, vel_o, st_o, mean_o, var_o, sem):
@@ -544,7 +550,7 @@
     hbm = pl.BlockSpec(memory_space=pltpu.HBM)
     vmem = pl.BlockSpec(memory_space=pltpu.VMEM)
     stat = jax.ShapeDtypeStruct((3, OWN, 2 * LANES), f32)
-    big = [pltpu.with_memory_space_constraint(x, pltpu.HBM) for x in (velocity, stress, thickness, concentration, node_mass, wind_stress, ocean_current, ocean_mask)]
+    big = [pltpu.with_memory_space_constraint(x, pltpu.HBM) for x in (velocity, stress, thickness, concentration, node_mass, wind_stress, ocean_current, ocean_mask, ice_blocks)]
     results = pl.pallas_call(
         kernel,
         out_shape=(
@@ -552,33 +558,34 @@
             jax.ShapeDtypeStruct((3, 2, ROWS, LANES), f32),
             jax.ShapeDtypeStruct((2, 3, 2, OWN, LANES), f32),
         ),
-        in_specs=[hbm] * 8 + [pl.BlockSpec(memory_space=pltpu.SMEM)],
+        in_specs=[hbm] * 9,
         out_specs=(vmem,) * 3,
         scratch_shapes=[
             pltpu.VMEM((14, 3, ALLOC, LANES), f32),
             pltpu.VMEM((5, 3, ALLOC, LANES), f32),
-            pltpu.VMEM((2, 10, 3, 48, LANES), f32),
-            pltpu.VMEM((12, 2, ROWS, LANES), f32),
+            pltpu.VMEM((2, 10, 3, 56, LANES), f32),
+            pltpu.VMEM((12, 2, ROWS + 8, LANES), f32),
             pltpu.VMEM((2, ROWS, LANES), jnp.int32),
             pltpu.VMEM((2, 2, ROWS, LANES), f32),
             pltpu.VMEM((2, 2, ROWS, LANES), f32),
-            pltpu.VMEM((10, 3, 8 * (CTILES + 2), LANES), f32),
-            pltpu.VMEM((2, 3, 3, 2, OWN, LANES), f32),
-            pltpu.VMEM((2, 2, 3, 2, OWN, LANES), f32),
-            pltpu.VMEM((2, 3, 2, OWN, LANES), f32),
-            pltpu.SemaphoreType.DMA((26,)),
+            pltpu.VMEM((10, 3, 16 * GROWS + 8, LANES), f32),
+            pltpu.VMEM((8, 3, 3, 2, 8, LANES), f32),
+            pltpu.VMEM((8, 2, 3, 2, 8, LANES), f32),
+            pltpu.VMEM((8, 2, 3, 2, 8, LANES), f32),
+            pltpu.SMEM((1, 8, 8), jnp.int32),
+            pltpu.SemaphoreType.DMA((52,)),
+            pltpu.SemaphoreType.DMA,
             pltpu.SemaphoreType.DMA((12,)),
             pltpu.SemaphoreType.DMA((12,)),
-            pltpu.SemaphoreType.DMA((6,)),
-            pltpu.SemaphoreType.DMA((6,)),
-            pltpu.SemaphoreType.DMA,
-            pltpu.SemaphoreType.DMA,
+            pltpu.SemaphoreType.DMA((24,)),
+            pltpu.SemaphoreType.DMA((24,)),
+            pltpu.SemaphoreType.DMA((8,)),
+            pltpu.SemaphoreType.DMA((8,)),
         ],
         compiler_params=pltpu.CompilerParams(
             collective_id=0, has_side_effects=True, vmem_limit_bytes=40 * 1024 * 1024),
         name="ice",
-    )(*big,
-      ice_blocks)
+    )(*big)
     return pl.pallas_call(
         emit,
         out_shape=(

time: 59 us -> 51.8 us (0.88)
  the two profiles are of different devices: /device:TPU:16 before, /device:TPU:192 now
where the time goes in v3:
time: 51.8 us; the launch traced here: 51.7 us
  Pallas kernels  51.1 us (99%)
  between operations  0.64 us (1%)
    pallas_call x1, Pallas kernels, body(): pl.pallas_call(kernel, out_shape=(jax.ShapeDtypeStruct((3, 2, ROWS, LANES...  49.8 us
    pallas_call x1, Pallas kernels, body(): pl.pallas_call(emit, out_shape=(jax.ShapeDtypeStruct(velocity.shape, f32)...  1.22 us

profile of v3, /device:TPU:192, one launch (start us, length us, event | category | flops | bytes accessed | tf_op | source)
XLA Modules:
  0.0 51.7 jit_solution(15117606039786384459)
XLA Ops:
  0.6 49.8 %ice.1 = (f32[3,2,256,128]{3,2,1,0:T(8,128)S(1)}, f32[3,2,256,128]{3,2,1,0:T(8,128)S(1)}, f32[2,3,2,32,128]{4,3,2,1,0:T(8,128)S(1)}) custom-call(f32[1,2,256,256]{3,2,1,0:T(8,128)} %vel_h.1, f32[1,3,256,256]{3,2,1,0:T(8,128)} %st_h.1, f32[1,256,256]{2,1,0:T(8,128)} %thick_h.1, f32[1,256,256]{2,1,0:T(8,128)} %conc_h.1, f32[1,256,256]{2,1,0:T(8,128)} %mass_h.1, ...), custom_call_target="tpu_custom_call" | custom-call | tf_op jit(solution)/shard_map/ice/pallas_call | solution.py:554
  50.5 1.2 %emit.1 = (f32[1,2,256,256]{3,2,1,0:T(8,128)}, f32[1,3,256,256]{3,2,1,0:T(8,128)}, f32[3,32,256]{2,1,0:T(8,128)}, f32[3,32,256]{2,1,0:T(8,128)}) custom-call(f32[3,2,256,128]{3,2,1,0:T(8,128)S(1)} %get-tuple-element.7.FB, f32[3,2,256,128]{3,2,1,0:T(8,128)S(1)} %get-tuple-element.8.OUT, f32[2,3,2,32,128]{4,3,2,1,0:T(8,128)S(1)} %get-tuple-element.9.STAT), custom_call_target="tpu_custom_call" | custom-call | tf_op jit(solution)/shard_map/emit/pallas_call | solution.py:589
